TPU v7x, 32 devices: a whole 2x2x4 slice. The times are simulated.
32 devices in a mesh: gx: 2 (over x), gy: 4 (over y, core), ha: 4 (over z).
Axes of the slice: x: 2, y: 2, z: 4, core: 2. Of those that a mesh axis runs over, the one named last changes fastest.
Arguments:
- global_state: float32 [8, 60, 16, 16], P(None, 'ha', 'gx', 'gy'), may hold values from -6 to 6
- crm_state: float32 [8, 60, 16, 1024], P(None, 'ha', 'gx', 'gy'), may hold values from -6 to 6
- mixing: float32 [8, 8], replicated, may hold values from -2 to 2
- substeps: int32 [16, 16], P('gx', 'gy'), may hold values from 1 to 8
- assignment: int32 [16, 16], P('gx', 'gy'), may hold values from 0 to 31, as said below
Outputs:
- new_global: float32 [8, 60, 16, 16], P(None, 'ha', 'gx', 'gy')
- new_crm: float32 [8, 60, 16384], P(None, None, ('gx', 'gy', 'ha'))
Inputs may be any that keep to these rules, and one draw needn't show every extreme that they name: `assignment`: within each tile of 8 x 4 columns every value 0 .. 31 appears once; value // 8 is the helper index, value % 8 the slot on that helper.
All inputs are finite; a program needn't handle non-finite values.
Results may differ from a plain program's by a relative error of at most 0.0003.
Values sent between devices are 32-bit elements; how exact they have to be, the bound alone decides.
A program may use at most 64 MiB of HBM per device.

v0:
```python
import functools

import jax
import jax.numpy as jnp
from jax import lax
from jax.experimental import pallas as pl
from jax.experimental.pallas import tpu as pltpu
from jax.sharding import PartitionSpec as P

MAXSUB = 8
GSUB = 4
LANES = 128
CHUNK = 30
MESH = pl.DeviceIdType.MESH
HIGH = lax.Precision.HIGHEST
F32 = jnp.float32
I32 = jnp.int32


def lane_iota(shape):
    return lax.broadcasted_iota(I32, shape, len(shape) - 1)


def expand_levels(v, lane, slots, p):
    v = jnp.where(lax.div(lax.rem(lane, slots), 2) == p, v, 0.0)
    if p > 0:
        v = pltpu.roll(v, LANES - 2 * p, 1)
    shift = 2
    while shift < slots:
        v = v + pltpu.roll(v, shift, 1)
        shift *= 2
    parts = [v]
    while shift < LANES:
        clear = (lane & shift) == 0
        low = [jnp.where(clear, u, pltpu.roll(u, shift, 1)) for u in parts]
        high = [jnp.where(clear, pltpu.roll(u, LANES - shift, 1), u) for u in parts]
        parts = low + high
        shift *= 2
    return parts


def fold_levels(parts, lane, slots):
    shift = LANES // 2
    while shift >= slots:
        clear = (lane & shift) == 0
        half = len(parts) // 2
        after = []
        for a, b in zip(parts[:half], parts[half:]):
            after.append(jnp.where(
                clear, a + pltpu.roll(a, LANES - shift, 1), b + pltpu.roll(b, shift, 1)))
        parts = after
        shift //= 2
    v = parts[0]
    while shift >= 2:
        v = v + jnp.where(
            (lane & shift) == 0, pltpu.roll(v, LANES - shift, 1), pltpu.roll(v, shift, 1))
        shift //= 2
    return v


def step_kernel(
    dims, sizes, assign_ref, steps_ref, mixing_ref, g_ref, crm_ref, out_ref, newg_ref,
    raw, slots_ref, state, work, done, push, packed_g, ext, diag, g4, fcol,
    fsend, frecv, tsend, trecv, mask, table_ref,
    raw_sem, out_sem, halo_send, halo_recv, crm_send, crm_recv, f_send, f_recv, t_send, t_recv,
):
    fields, levels, tile_x, tile_y, width, helpers, pairs = dims
    n_gx, n_gy = sizes
    columns = tile_x * tile_y
    levels_all = levels * helpers
    slots = 2 * pairs
    span = LANES // tile_y
    h = GSUB
    gx, gy, ha = lax.axis_index("gx"), lax.axis_index("gy"), lax.axis_index("ha")

    offsets = [(dx, dy) for dx in (0, 1, -1) for dy in (0, 1, -1) if (dx, dy) != (0, 0)]

    def tile_at(dx, dy):
        return {"gx": lax.rem(gx + dx + n_gx, n_gx), "gy": lax.rem(gy + dy + n_gy, n_gy)}

    order = sorted(range(1, helpers), key=lambda i: -min(i, helpers - i))
    peers = [lax.rem(ha + i, helpers) for i in order]
    barrier = pltpu.get_barrier_semaphore()
    for peer in peers:
        pl.semaphore_signal(barrier, inc=1, device_id={"ha": peer}, device_id_type=MESH)
    for dx, dy in offsets:
        pl.semaphore_signal(barrier, inc=1, device_id=tile_at(dx, dy), device_id_type=MESH)
    halves = raw.shape[0]
    loads = [
        pltpu.make_async_copy(
            crm_ref.at[:, pl.ds(LANES * i, LANES)], raw.at[i], raw_sem.at[i])
        for i in range(halves)
    ]
    for copy in loads:
        copy.start()

    def find(v, carry):
        found = 0
        for x in range(tile_x):
            for y in range(tile_y):
                found = jnp.where(assign_ref[y, x] == v, x * tile_y + y, found)
        table_ref[v] = found
        table_ref[columns + v] = steps_ref[lax.rem(found, tile_y), lax.div(found, tile_y)]
        return carry

    lax.fori_loop(0, columns, find, 0)

    packed_g[...] = jnp.zeros(packed_g.shape, F32)
    for x in range(tile_x):
        for y in range(tile_y):
            packed_g[x, :, y * span:y * span + levels] = g_ref[
                pl.ds(x * tile_y + y, fields, stride=columns), :]

    lane = lane_iota((fields, LANES))
    even = lax.rem(lane, 2) == 0
    half = lax.div(lane, 2)

    def gather(q):
        ca = table_ref[2 * q]
        cb = table_ref[2 * q + 1]
        xa, ya = lax.div(ca, tile_y), lax.rem(ca, tile_y)
        xb, yb = lax.div(cb, tile_y), lax.rem(cb, tile_y)
        ia = half + lax.rem(ya, 2) * width
        ib = half + lax.rem(yb, 2) * width
        ha_, hb_ = lax.div(ya, 2), lax.div(yb, 2)
        pieces = []
        for l in range(levels):
            a = raw[ha_, pl.ds(l * tile_x + xa, fields, stride=levels * tile_x), :]
            b = raw[hb_, pl.ds(l * tile_x + xb, fields, stride=levels * tile_x), :]
            a = jnp.take_along_axis(a, ia, axis=1)
            b = jnp.take_along_axis(b, ib, axis=1)
            pieces.append(jnp.where(even, a, b))
        return pieces

    def gather_pair(p):
        for peer in peers:
            for l, piece in enumerate(gather(peer * pairs + p)):
                slots_ref[(peer * pairs + p) * levels + l] = piece

    moves = []
    for p in range(pairs):
        row = []
        for i, peer in enumerate(peers):
            row.append(pltpu.make_async_remote_copy(
                src_ref=slots_ref.at[pl.ds((peer * pairs + p) * levels, levels)],
                dst_ref=state.at[p, pl.ds(ha * levels, levels)],
                send_sem=crm_send.at[p, i], recv_sem=crm_recv.at[p, i],
                device_id={"ha": peer}, device_id_type=MESH))
        moves.append(row)

    for copy in loads:
        copy.wait()
    gather_pair(0)
    pl.semaphore_wait(barrier, len(offsets) + len(peers))
    for copy in moves[0]:
        copy.start()

    halos = []
    for o, (dx, dy) in enumerate(offsets):
        if dx == 0:
            src, dst = packed_g, ext.at[1 - dy, pl.ds(h, tile_x)]
        elif dx == 1:
            src, dst = packed_g.at[pl.ds(tile_x - h, h)], ext.at[1 - dy, pl.ds(0, h)]
        else:
            src, dst = packed_g.at[pl.ds(0, h)], ext.at[1 - dy, pl.ds(tile_x + h, h)]
        halos.append(pltpu.make_async_remote_copy(
            src_ref=src, dst_ref=dst, send_sem=halo_send.at[o], recv_sem=halo_recv.at[o],
            device_id=tile_at(dx, dy), device_id_type=MESH))
        halos[-1].start()

    for p in range(1, pairs):
        gather_pair(p)
    for p in range(pairs):
        for l, piece in enumerate(gather(ha * pairs + p)):
            state[p, ha * levels + l] = piece
    ext[1, h:h + tile_x] = packed_g[...]
    lane3 = lane_iota((1, 1, LANES))
    for copy in halos:
        copy.wait_recv()
    tiles = [ext[t] for t in range(3)]
    for _ in range(GSUB):
        up = [pltpu.roll(t, LANES - span, 2) for t in tiles]
        down = [pltpu.roll(t, span, 2) for t in tiles]
        after = []
        for t in range(3):
            north = jnp.where(lane3 < LANES - span, up[t], up[min(t + 1, 2)])
            south = jnp.where(lane3 >= span, down[t], down[max(t - 1, 0)])
            v = tiles[t]
            after.append(
                0.6 * v[1:-1] + 0.025 * (v[2:] + north[1:-1]) + 0.175 * (v[:-2] + south[1:-1]))
        tiles = after
    g4[...] = tiles[1]
    forcing = (tiles[1] - packed_g[...]) * (1.0 / (0.5 * GSUB))

    rows = lax.broadcasted_iota(I32, (LANES, LANES), 0)
    cols = lax.broadcasted_iota(I32, (LANES, LANES), 1)
    flat = forcing.reshape(tile_x * fields, LANES)
    for y in range(tile_y):
        spread = jnp.where(rows == y * span + lax.div(cols, slots), 1.0, 0.0).astype(F32)
        fcol[y] = jnp.dot(flat, spread, precision=HIGH, preferred_element_type=F32).reshape(
            tile_x, fields, LANES)
    slot_of = lax.rem(lane, slots)
    for k in range(helpers):
        packed = jnp.zeros((fields, LANES), F32)
        for j in range(slots):
            c = table_ref[k * slots + j]
            v = fcol[lax.rem(c, tile_y), lax.div(c, tile_y)]
            packed = jnp.where(slot_of == j, v, packed)
        fsend[k] = packed
    fmoves = []
    for i, peer in enumerate(peers):
        fmoves.append(pltpu.make_async_remote_copy(
            src_ref=fsend.at[peer], dst_ref=frecv.at[ha],
            send_sem=f_send.at[i], recv_sem=f_recv.at[i],
            device_id={"ha": peer}, device_id_type=MESH))
        fmoves[-1].start()
    for p in range(1, pairs):
        for copy in moves[p]:
            copy.start()
    frecv[ha] = fsend[ha]

    mix = mixing_ref[...]
    mrow = lax.broadcasted_iota(I32, (fields, fields), 0)
    mcol = lax.broadcasted_iota(I32, (fields, fields), 1)
    for k in range(fields):
        picked = jnp.where(mcol == lax.rem(mrow + k, fields), mix, 0.0)
        diag[k] = jnp.broadcast_to(
            0.1 * jnp.sum(picked, axis=1, keepdims=True), (fields, LANES))
    chunk = max(d for d in range(1, CHUNK + 1) if levels_all % d == 0)

    for copy in fmoves:
        copy.wait_recv()
    pair_of = lax.div(lax.rem(lane, slots), 2)
    for p in range(pairs):
        for z in range(helpers):
            parts = expand_levels(0.1 * frecv[z], lane, slots, p)
            for l in range(levels):
                push[p, z * levels + l] = parts[l]

    unweave = 2 * lax.rem(lane, width) + lax.div(lane, width)
    sums = [jnp.zeros((fields, LANES), F32)] * helpers
    stores = []
    for p in range(pairs):
        for copy in moves[p]:
            copy.wait_recv()
        first = ha * slots + 2 * p
        counts = jnp.where(even, table_ref[columns + first], table_ref[columns + first + 1])

        def one_step(k, source, p=p, counts=counts):
            active = k < counts

            def some_levels(b, prev):
                l0 = b * chunk
                v = [prev] + [source[p, l0 + i] for i in range(chunk)]
                v.append(source[p, jnp.minimum(l0 + chunk, levels_all - 1)])
                for i in range(chunk):
                    s = v[i + 1]
                    t = jnp.tanh(s)
                    total = diag[0] * t + push[p, l0 + i]
                    for m in range(1, fields):
                        total = total + diag[m] * pltpu.roll(t, fields - m, 0)
                    total = total + 0.1 * (pltpu.roll(s, 2, 1) + pltpu.roll(s, LANES - 2, 1))
                    total = total + 0.05 * (v[i] + v[i + 2]) + 0.7 * s
                    work[p, l0 + i] = jnp.where(active, total, s)
                return v[chunk]

            lax.fori_loop(0, levels_all // chunk, some_levels, source[p, 0])

        def later_step(k, carry):
            one_step(k, work)
            return carry

        one_step(0, state)
        lax.fori_loop(1, MAXSUB, later_step, 0)
        zero = jnp.zeros((fields, LANES), F32)
        for z in range(helpers):
            parts = [work[p, z * levels + l] - state[p, z * levels + l] for l in range(levels)]
            parts += [zero] * (LANES // slots - levels)
            sums[z] = jnp.where(pair_of == p, fold_levels(parts, lane, slots), sums[z])
        if p == pairs - 1:
            for z in range(helpers):
                tsend[z] = sums[z]
            tmoves = []
            for i, peer in enumerate(peers):
                tmoves.append(pltpu.make_async_remote_copy(
                    src_ref=tsend.at[peer], dst_ref=trecv.at[ha],
                    send_sem=t_send.at[i], recv_sem=t_recv.at[i],
                    device_id={"ha": peer}, device_id_type=MESH))
                tmoves[-1].start()
            trecv[ha] = tsend[ha]
        for l in range(levels_all):
            done[p, l] = jnp.take_along_axis(work[p, l], unweave, axis=1)
        stores.append(pltpu.make_async_copy(
            done.at[p], out_ref.at[:, :, pl.ds(p * LANES, LANES)], out_sem.at[p]))
        stores[-1].start()

    for row in moves:
        for copy in row:
            copy.wait_send()
    for copy in halos + fmoves:
        copy.wait_send()
    for copy in tmoves:
        copy.wait()
    placed = jnp.zeros((tile_x * fields, LANES), F32)
    for y in range(tile_y):
        for x in range(tile_x):
            a = assign_ref[y, x]
            v = trecv[lax.div(a, slots)]
            mask[x] = jnp.where(slot_of == lax.rem(a, slots), v, 0.0)
        pick = jnp.where(
            (cols == y * span + lax.div(rows, slots)) & (rows < levels * slots), 1.0, 0.0
        ).astype(F32)
        placed = placed + jnp.dot(
            mask[...].reshape(tile_x * fields, LANES), pick,
            precision=HIGH, preferred_element_type=F32)
    newg = g4[...] + (1.0 / width) * placed.reshape(tile_x, fields, LANES)
    for x in range(tile_x):
        for y in range(tile_y):
            newg_ref[pl.ds(x * tile_y + y, fields, stride=columns), :] = (
                newg[x][:, y * span:y * span + levels])
    for copy in stores:
        copy.wait()


def on_device(sizes, global_state, crm_state, mixing, substeps, assignment):
    n_gx, n_gy, helpers = sizes
    fields, levels = crm_state.shape[:2]
    tile_x, tile_y = assignment.shape
    width = crm_state.shape[3] // tile_y
    columns = tile_x * tile_y
    per_helper = columns // helpers
    pairs = per_helper // 2
    span = LANES // tile_y
    levels_all = levels * helpers
    assert 2 * width == LANES and tile_y == 4 and fields == 8
    assert LANES % per_helper == 0 and levels <= LANES // per_helper and levels <= span
    assert tile_x >= GSUB and tile_y >= GSUB
    dims = (fields, levels, tile_x, tile_y, width, helpers, pairs)

    g = jnp.transpose(global_state, (0, 2, 3, 1)).reshape(fields * columns, levels)
    rows = fields * levels * tile_x
    flat = crm_state.reshape(rows, tile_y * width)

    smem = pl.BlockSpec(memory_space=pltpu.SMEM)
    vmem = pl.BlockSpec(memory_space=pltpu.VMEM)
    anywhere = pl.BlockSpec(memory_space=pl.ANY)
    dma = pltpu.SemaphoreType.DMA
    vec = (fields, LANES)
    peers = helpers - 1
    new_crm, newg = pl.pallas_call(
        functools.partial(step_kernel, dims, (n_gx, n_gy)),
        out_shape=(
            jax.ShapeDtypeStruct((levels_all, fields, per_helper * width), F32),
            jax.ShapeDtypeStruct((fields * columns, levels), F32),
        ),
        in_specs=[smem, smem, vmem, vmem, anywhere],
        out_specs=(anywhere, vmem),
        scratch_shapes=[
            pltpu.VMEM((tile_y * width // LANES, rows, LANES), F32),
            pltpu.VMEM((helpers * pairs * levels,) + vec, F32),
            pltpu.VMEM((pairs, levels_all) + vec, F32),
            pltpu.VMEM((pairs, levels_all) + vec, F32),
            pltpu.VMEM((pairs, levels_all) + vec, F32),
            pltpu.VMEM((pairs, levels_all) + vec, F32),
            pltpu.VMEM((tile_x,) + vec, F32),
            pltpu.VMEM((3, tile_x + 2 * GSUB) + vec, F32),
            pltpu.VMEM((fields,) + vec, F32),
            pltpu.VMEM((tile_x,) + vec, F32),
            pltpu.VMEM((tile_y, tile_x) + vec, F32),
            pltpu.VMEM((helpers,) + vec, F32),
            pltpu.VMEM((helpers,) + vec, F32),
            pltpu.VMEM((helpers,) + vec, F32),
            pltpu.VMEM((helpers,) + vec, F32),
            pltpu.VMEM((tile_x,) + vec, F32),
            pltpu.SMEM((2 * columns,), I32),
            dma((tile_y * width // LANES,)), dma((pairs,)),
            dma((8,)), dma((8,)),
            dma((pairs, peers)), dma((pairs, peers)),
            dma((peers,)), dma((peers,)),
            dma((peers,)), dma((peers,)),
        ],
        compiler_params=pltpu.CompilerParams(collective_id=0, has_side_effects=True),
    )(assignment.T, substeps.T, mixing, g, flat)

    newg = newg.reshape(fields, tile_x, tile_y, levels)
    return jnp.transpose(newg, (0, 3, 1, 2)), jnp.transpose(new_crm, (1, 0, 2))


def solution(mesh):
    sizes = (mesh.shape["gx"], mesh.shape["gy"], mesh.shape["ha"])
    in_specs = (
        P(None, "ha", "gx", "gy"),
        P(None, "ha", "gx", "gy"),
        P(),
        P("gx", "gy"),
        P("gx", "gy"),
    )
    out_specs = (P(None, "ha", "gx", "gy"), P(None, None, ("gx", "gy", "ha")))
    return jax.shard_map(
        functools.partial(on_device, sizes),
        mesh=mesh, in_specs=in_specs, out_specs=out_specs, check_vma=False,
    )
```

profile of v0, /device:TPU:0, one launch (start us, length us, event | category | flops | bytes accessed | tf_op | source)
XLA Modules:
  0.0 41.5 jit_solution(11099850151208581387)
XLA Ops:
  0.6 37.0 %shard_map.68 = (f32[60,8,512]{2,1,0:T(8,128)}, f32[256,15]{1,0:T(8,128)}) custom-call(s32[4,8]{1,0:T(4,128)} %bitcast.14, s32[4,8]{1,0:T(4,128)} %bitcast.15, f32[8,8]{1,0:T(8,128)} %mixing_ref.1, f32[256,15]{1,0:T(8,128)} %bitcast.12, f32[960,256]{1,0:T(8,128)} %bitcast.10), custom_call_target="tpu_custom_call" | custom-call | tf_op jit(solution)/shard_map/pallas_call | solution.py:350
  37.7 1.6 %copy.9 = f32[8,15,8,4]{1,3,2,0:T(4,128)} copy(f32[8,15,8,4]{1,3,2,0:T(4,128)} %bitcast.13) | data formatting | bytes 30720
  39.2 2.2 %copy.10 = f32[8,60,512]{2,0,1:T(8,128)} copy(f32[8,60,512]{2,0,1:T(8,128)} %bitcast.11) | data formatting | bytes 1966080
where the time goes:
time: 41.7 us; the launch traced here: 41.5 us
  Pallas kernels  37 us (89%)
  local copies, waits for them, and re-layouts  3.78 us (9%)
  between operations  0.64 us (2%)
    pallas_call x1, Pallas kernels, on_device(): pl.pallas_call(functools.partial(step_kernel, dims, (n_gx, n_gy)), out_sh...  37 us
    unnamed x2, local copies, waits for them, and re-layouts  3.78 us

commit v1 on v0

--- a/solution.py
+++ b/solution.py
@@ -10,10 +10,11 @@
 MAXSUB = 8
 GSUB = 4
 LANES = 128
-CHUNK = 30
+GROUP = 10
 MESH = pl.DeviceIdType.MESH
 HIGH = lax.Precision.HIGHEST
 F32 = jnp.float32
+BF16 = jnp.bfloat16
 I32 = jnp.int32
 
 
@@ -58,16 +59,21 @@
     return v
 
 
+def group_of(levels_all):
+    return max(d for d in range(2, GROUP + 1, 2) if levels_all % d == 0)
+
+
 def step_kernel(
     dims, sizes, assign_ref, steps_ref, mixing_ref, g_ref, crm_ref, out_ref, newg_ref,
-    raw, slots_ref, state, work, done, push, packed_g, ext, diag, g4, fcol,
-    fsend, frecv, tsend, trecv, mask, table_ref,
-    raw_sem, out_sem, halo_send, halo_recv, crm_send, crm_recv, f_send, f_recv, t_send, t_recv,
+    raw, slots_ref, state, one, two, push, packed_g, ext, coupling, g4, fcol,
+    fsend, frecv, tsend, trecv, table_ref,
+    raw_sem, halo_send, halo_recv, crm_send, crm_recv, f_send, f_recv, t_send, t_recv,
 ):
     fields, levels, tile_x, tile_y, width, helpers, pairs = dims
     n_gx, n_gy = sizes
     columns = tile_x * tile_y
     levels_all = levels * helpers
+    group = group_of(levels_all)
     slots = 2 * pairs
     span = LANES // tile_y
     h = GSUB
@@ -94,22 +100,23 @@
     for copy in loads:
         copy.start()
 
-    def find(v, carry):
+    def find(v):
         found = 0
         for x in range(tile_x):
             for y in range(tile_y):
                 found = jnp.where(assign_ref[y, x] == v, x * tile_y + y, found)
         table_ref[v] = found
         table_ref[columns + v] = steps_ref[lax.rem(found, tile_y), lax.div(found, tile_y)]
+
+    def find_first(i, carry):
+        find(lax.div(i, 2) * slots + lax.rem(i, 2))
         return carry
 
-    lax.fori_loop(0, columns, find, 0)
-
-    packed_g[...] = jnp.zeros(packed_g.shape, F32)
-    for x in range(tile_x):
-        for y in range(tile_y):
-            packed_g[x, :, y * span:y * span + levels] = g_ref[
-                pl.ds(x * tile_y + y, fields, stride=columns), :]
+    def find_other(i, carry):
+        find(lax.div(i, slots - 2) * slots + 2 + lax.rem(i, slots - 2))
+        return carry
+
+    lax.fori_loop(0, 2 * helpers, find_first, 0)
 
     lane = lane_iota((fields, LANES))
     even = lax.rem(lane, 2) == 0
@@ -137,16 +144,15 @@
             for l, piece in enumerate(gather(peer * pairs + p)):
                 slots_ref[(peer * pairs + p) * levels + l] = piece
 
-    moves = []
-    for p in range(pairs):
-        row = []
-        for i, peer in enumerate(peers):
-            row.append(pltpu.make_async_remote_copy(
-                src_ref=slots_ref.at[pl.ds((peer * pairs + p) * levels, levels)],
-                dst_ref=state.at[p, pl.ds(ha * levels, levels)],
-                send_sem=crm_send.at[p, i], recv_sem=crm_recv.at[p, i],
-                device_id={"ha": peer}, device_id_type=MESH))
-        moves.append(row)
+    def crm_move(p, peer, lands):
+        return pltpu.make_async_remote_copy(
+            src_ref=slots_ref.at[pl.ds((peer * pairs + p) * levels, levels)],
+            dst_ref=state.at[p, pl.ds(lands * levels, levels)],
+            send_sem=crm_send.at[p, peer], recv_sem=crm_recv.at[p, lands],
+            device_id={"ha": peer}, device_id_type=MESH)
+
+    moves = [[crm_move(p, peer, ha) for peer in peers] for p in range(pairs)]
+    arrivals = [[crm_move(p, peer, peer) for peer in peers] for p in range(pairs)]
 
     for copy in loads:
         copy.wait()
@@ -154,6 +160,12 @@
     pl.semaphore_wait(barrier, len(offsets) + len(peers))
     for copy in moves[0]:
         copy.start()
+
+    packed_g[...] = jnp.zeros(packed_g.shape, F32)
+    for x in range(tile_x):
+        for y in range(tile_y):
+            packed_g[x, :, y * span:y * span + levels] = g_ref[
+                pl.ds(x * tile_y + y, fields, stride=columns), :]
 
     halos = []
     for o, (dx, dy) in enumerate(offsets):
@@ -168,6 +180,7 @@
             device_id=tile_at(dx, dy), device_id_type=MESH))
         halos[-1].start()
 
+    lax.fori_loop(0, columns - 2 * helpers, find_other, 0)
     for p in range(1, pairs):
         gather_pair(p)
     for p in range(pairs):
@@ -189,7 +202,9 @@
             after.append(
                 0.6 * v[1:-1] + 0.025 * (v[2:] + north[1:-1]) + 0.175 * (v[:-2] + south[1:-1]))
         tiles = after
-    g4[...] = tiles[1]
+    for x in range(tile_x):
+        for y in range(tile_y):
+            g4[x * tile_y + y] = pltpu.roll(tiles[1][x], (LANES - y * span) % LANES, 1)
     forcing = (tiles[1] - packed_g[...]) * (1.0 / (0.5 * GSUB))
 
     rows = lax.broadcasted_iota(I32, (LANES, LANES), 0)
@@ -220,13 +235,22 @@
     frecv[ha] = fsend[ha]
 
     mix = mixing_ref[...]
-    mrow = lax.broadcasted_iota(I32, (fields, fields), 0)
-    mcol = lax.broadcasted_iota(I32, (fields, fields), 1)
-    for k in range(fields):
-        picked = jnp.where(mcol == lax.rem(mrow + k, fields), mix, 0.0)
-        diag[k] = jnp.broadcast_to(
-            0.1 * jnp.sum(picked, axis=1, keepdims=True), (fields, LANES))
-    chunk = max(d for d in range(1, CHUNK + 1) if levels_all % d == 0)
+    height = group * fields
+    tall = lax.broadcasted_iota(I32, (height, fields), 0)
+    pick_row = jnp.where(
+        lax.rem(tall, fields) == lax.broadcasted_iota(I32, (height, fields), 1), 1.0, 0.0)
+    flat_row = lax.broadcasted_iota(I32, (fields, 3 * height), 0)
+    flat_col = lax.broadcasted_iota(I32, (fields, 3 * height), 1)
+    pick_col = jnp.where(lax.rem(flat_col, fields) == flat_row, 1.0, 0.0)
+    spread_mix = jnp.dot(
+        jnp.dot(pick_row.astype(F32), 0.1 * mix, precision=HIGH, preferred_element_type=F32),
+        pick_col.astype(F32), precision=HIGH, preferred_element_type=F32)
+    block_row = lax.broadcasted_iota(I32, (height, 3 * height), 0)
+    block_col = lax.broadcasted_iota(I32, (height, 3 * height), 1)
+    same = lax.div(block_row, fields) == lax.rem(lax.div(block_col, fields), group)
+    spread_mix = jnp.where(same, spread_mix, 0.0)
+    top = spread_mix.astype(BF16).astype(F32)
+    coupling[...] = jnp.where(block_col < 2 * height, top, spread_mix - top).astype(BF16)
 
     for copy in fmoves:
         copy.wait_recv()
@@ -239,43 +263,57 @@
 
     unweave = 2 * lax.rem(lane, width) + lax.div(lane, width)
     sums = [jnp.zeros((fields, LANES), F32)] * helpers
-    stores = []
     for p in range(pairs):
-        for copy in moves[p]:
+        for copy in arrivals[p]:
             copy.wait_recv()
         first = ha * slots + 2 * p
         counts = jnp.where(even, table_ref[columns + first], table_ref[columns + first + 1])
 
-        def one_step(k, source, p=p, counts=counts):
+        def advance(k, read, emit, p=p, counts=counts):
             active = k < counts
-
-            def some_levels(b, prev):
-                l0 = b * chunk
-                v = [prev] + [source[p, l0 + i] for i in range(chunk)]
-                v.append(source[p, jnp.minimum(l0 + chunk, levels_all - 1)])
-                for i in range(chunk):
-                    s = v[i + 1]
-                    t = jnp.tanh(s)
-                    total = diag[0] * t + push[p, l0 + i]
-                    for m in range(1, fields):
-                        total = total + diag[m] * pltpu.roll(t, fields - m, 0)
-                    total = total + 0.1 * (pltpu.roll(s, 2, 1) + pltpu.roll(s, LANES - 2, 1))
-                    total = total + 0.05 * (v[i] + v[i + 2]) + 0.7 * s
-                    work[p, l0 + i] = jnp.where(active, total, s)
-                return v[chunk]
-
-            lax.fori_loop(0, levels_all // chunk, some_levels, source[p, 0])
-
-        def later_step(k, carry):
-            one_step(k, work)
+            for g in range(levels_all // group):
+                l0 = g * group
+                t = jnp.concatenate([jnp.tanh(read(l0 + i)) for i in range(group)], axis=0)
+                upper = t.astype(BF16)
+                lower = (t - upper.astype(F32)).astype(BF16)
+                mixed = jnp.dot(
+                    coupling[...], jnp.concatenate([upper, lower, upper], axis=0),
+                    preferred_element_type=F32)
+                for i in range(group):
+                    l = l0 + i
+                    s = read(l)
+                    near = read(max(l - 1, 0)) + read(min(l + 1, levels_all - 1))
+                    side = pltpu.roll(s, 2, 1) + pltpu.roll(s, LANES - 2, 1)
+                    total = mixed[i * fields:(i + 1) * fields] + push[p, l]
+                    total = total + 0.1 * side + (0.05 * near + 0.7 * s)
+                    emit(l, jnp.where(active, total, s))
+
+        def hold(ref):
+            def store(l, v):
+                ref[l] = v
+            return store
+
+        def two_steps(i, carry):
+            advance(2 * i + 1, lambda l: one[l], hold(two))
+            advance(2 * i + 2, lambda l: two[l], hold(one))
             return carry
 
-        one_step(0, state)
-        lax.fori_loop(1, MAXSUB, later_step, 0)
+        grown = []
+
+        def finish(l, v, p=p):
+            two[l] = v
+            grown.append(v - state[p, l])
+
+        advance(0, lambda l: state[p, l], hold(one))
+        if p < pairs - 1:
+            lax.fori_loop(0, MAXSUB // 2 - 1, two_steps, 0)
+        else:
+            for i in range(MAXSUB // 2 - 1):
+                two_steps(i, 0)
+        advance(MAXSUB - 1, lambda l: one[l], finish)
         zero = jnp.zeros((fields, LANES), F32)
         for z in range(helpers):
-            parts = [work[p, z * levels + l] - state[p, z * levels + l] for l in range(levels)]
-            parts += [zero] * (LANES // slots - levels)
+            parts = grown[z * levels:(z + 1) * levels] + [zero] * (LANES // slots - levels)
             sums[z] = jnp.where(pair_of == p, fold_levels(parts, lane, slots), sums[z])
         if p == pairs - 1:
             for z in range(helpers):
@@ -289,10 +327,8 @@
                 tmoves[-1].start()
             trecv[ha] = tsend[ha]
         for l in range(levels_all):
-            done[p, l] = jnp.take_along_axis(work[p, l], unweave, axis=1)
-        stores.append(pltpu.make_async_copy(
-            done.at[p], out_ref.at[:, :, pl.ds(p * LANES, LANES)], out_sem.at[p]))
-        stores[-1].start()
+            out_ref[l, :, p * LANES:(p + 1) * LANES] = jnp.take_along_axis(
+                two[l], unweave, axis=1)
 
     for row in moves:
         for copy in row:
@@ -301,24 +337,24 @@
         copy.wait_send()
     for copy in tmoves:
         copy.wait()
-    placed = jnp.zeros((tile_x * fields, LANES), F32)
-    for y in range(tile_y):
-        for x in range(tile_x):
-            a = assign_ref[y, x]
-            v = trecv[lax.div(a, slots)]
-            mask[x] = jnp.where(slot_of == lax.rem(a, slots), v, 0.0)
-        pick = jnp.where(
-            (cols == y * span + lax.div(rows, slots)) & (rows < levels * slots), 1.0, 0.0
-        ).astype(F32)
-        placed = placed + jnp.dot(
-            mask[...].reshape(tile_x * fields, LANES), pick,
-            precision=HIGH, preferred_element_type=F32)
-    newg = g4[...] + (1.0 / width) * placed.reshape(tile_x, fields, LANES)
     for x in range(tile_x):
         for y in range(tile_y):
-            newg_ref[pl.ds(x * tile_y + y, fields, stride=columns), :] = (
-                newg[x][:, y * span:y * span + levels])
-    for copy in stores:
+            c = x * tile_y + y
+            a = assign_ref[y, x]
+            where = jnp.minimum(lane * slots + lax.rem(a, slots), LANES - 1)
+            mean = (1.0 / width) * jnp.take_along_axis(trecv[lax.div(a, slots)], where, axis=1)
+            newg_ref[pl.ds(c, fields, stride=columns), :] = (g4[c] + mean)[:, :levels]
+
+
+def write_kernel(pieces, crm_ref, newg_ref, crm_out, newg_out, sem):
+    step = crm_ref.shape[0] // pieces
+    copies = [pltpu.make_async_copy(newg_ref, newg_out, sem.at[pieces])]
+    for i in range(pieces):
+        rows = pl.ds(i * step, step)
+        copies.append(pltpu.make_async_copy(crm_ref.at[rows], crm_out.at[rows], sem.at[i]))
+    for copy in copies:
+        copy.start()
+    for copy in copies:
         copy.wait()
 
 
@@ -335,7 +371,9 @@
     assert 2 * width == LANES and tile_y == 4 and fields == 8
     assert LANES % per_helper == 0 and levels <= LANES // per_helper and levels <= span
     assert tile_x >= GSUB and tile_y >= GSUB
+    assert levels_all % 2 == 0 and MAXSUB % 2 == 0
     dims = (fields, levels, tile_x, tile_y, width, helpers, pairs)
+    group = group_of(levels_all)
 
     g = jnp.transpose(global_state, (0, 2, 3, 1)).reshape(fields * columns, levels)
     rows = fields * levels * tile_x
@@ -350,37 +388,48 @@
     new_crm, newg = pl.pallas_call(
         functools.partial(step_kernel, dims, (n_gx, n_gy)),
         out_shape=(
-            jax.ShapeDtypeStruct((levels_all, fields, per_helper * width), F32),
-            jax.ShapeDtypeStruct((fields * columns, levels), F32),
+            pltpu.VMEM((levels_all, fields, per_helper * width), F32),
+            pltpu.VMEM((fields * columns, levels), F32),
         ),
         in_specs=[smem, smem, vmem, vmem, anywhere],
-        out_specs=(anywhere, vmem),
+        out_specs=(vmem, vmem),
         scratch_shapes=[
             pltpu.VMEM((tile_y * width // LANES, rows, LANES), F32),
             pltpu.VMEM((helpers * pairs * levels,) + vec, F32),
             pltpu.VMEM((pairs, levels_all) + vec, F32),
-            pltpu.VMEM((pairs, levels_all) + vec, F32),
-            pltpu.VMEM((pairs, levels_all) + vec, F32),
+            pltpu.VMEM((levels_all,) + vec, F32),
+            pltpu.VMEM((levels_all,) + vec, F32),
             pltpu.VMEM((pairs, levels_all) + vec, F32),
             pltpu.VMEM((tile_x,) + vec, F32),
             pltpu.VMEM((3, tile_x + 2 * GSUB) + vec, F32),
-            pltpu.VMEM((fields,) + vec, F32),
-            pltpu.VMEM((tile_x,) + vec, F32),
+            pltpu.VMEM((group * fields, 3 * group * fields), BF16),
+            pltpu.VMEM((columns,) + vec, F32),
             pltpu.VMEM((tile_y, tile_x) + vec, F32),
             pltpu.VMEM((helpers,) + vec, F32),
             pltpu.VMEM((helpers,) + vec, F32),
             pltpu.VMEM((helpers,) + vec, F32),
             pltpu.VMEM((helpers,) + vec, F32),
-            pltpu.VMEM((tile_x,) + vec, F32),
             pltpu.SMEM((2 * columns,), I32),
-            dma((tile_y * width // LANES,)), dma((pairs,)),
+            dma((tile_y * width // LANES,)),
             dma((8,)), dma((8,)),
-            dma((pairs, peers)), dma((pairs, peers)),
+            dma((pairs, helpers)), dma((pairs, helpers)),
             dma((peers,)), dma((peers,)),
             dma((peers,)), dma((peers,)),
         ],
         compiler_params=pltpu.CompilerParams(collective_id=0, has_side_effects=True),
     )(assignment.T, substeps.T, mixing, g, flat)
+
+    pieces = 4 if levels_all % 4 == 0 else 1
+    new_crm, newg = pl.pallas_call(
+        functools.partial(write_kernel, pieces),
+        out_shape=(
+            jax.ShapeDtypeStruct((levels_all, fields, per_helper * width), F32),
+            jax.ShapeDtypeStruct((fields * columns, levels), F32),
+        ),
+        in_specs=[anywhere, anywhere],
+        out_specs=(anywhere, anywhere),
+        scratch_shapes=[dma((pieces + 1,))],
+    )(pltpu.with_memory_space_constraint(new_crm, pltpu.VMEM), pltpu.with_memory_space_constraint(newg, pltpu.VMEM))
 
     newg = newg.reshape(fields, tile_x, tile_y, levels)
     return jnp.transpose(newg, (0, 3, 1, 2)), jnp.transpose(new_crm, (1, 0, 2))

time: 41.7 us -> 36.9 us (0.88)
  local copies, waits for them, and re-layouts: 3.78 us -> 0 us
  Pallas kernels: 37 us -> 36.1 us
    unnamed x2 -> x0, local copies, waits for them, and re-layouts: 3.78 us -> none
    pallas_call x1, Pallas kernels: 37 us -> 35 us  [on_device(): pl.pallas_call(functools.partial(step_kernel, dims, (n_gx, n_gy)), out_sh...]
    pallas_call x0 -> x1, Pallas kernels: none -> 1.02 us  [on_device(): pl.pallas_call(functools.partial(write_kernel, pieces), out_shape=(jax.Sh...]
where the time goes in v1:
time: 36.9 us; the launch traced here: 36.7 us
  Pallas kernels  36.1 us (98%)
  between operations  0.64 us (2%)
    pallas_call x1, Pallas kernels, on_device(): pl.pallas_call(functools.partial(step_kernel, dims, (n_gx, n_gy)), out_sh...  35 us
    pallas_call x1, Pallas kernels, on_device(): pl.pallas_call(functools.partial(write_kernel, pieces), out_shape=(jax.Sh...  1.02 us

profile of v1, /device:TPU:0, one launch (start us, length us, event | category | flops | bytes accessed | tf_op | source)
XLA Modules:
  0.0 36.7 jit_solution(6931673481352075411)
XLA Ops:
  0.6 35.0 %shard_map.68 = (f32[60,8,512]{2,1,0:T(8,128)S(1)}, f32[256,15]{1,0:T(8,128)S(1)}) custom-call(s32[4,8]{1,0:T(4,128)} %bitcast.12, s32[4,8]{1,0:T(4,128)} %bitcast.13, f32[8,8]{1,0:T(8,128)} %mixing_ref.1, f32[256,15]{1,0:T(8,128)} %bitcast.11, f32[960,256]{1,0:T(8,128)} %bitcast.10), custom_call_target="tpu_custom_call" | custom-call | tf_op jit(solution)/shard_map/pallas_call | solution.py:388
  35.7 1.0 %shard_map.69 = (f32[60,8,512]{2,1,0:T(8,128)}, f32[256,15]{1,0:T(8,128)}) custom-call(f32[60,8,512]{2,1,0:T(8,128)S(1)} %get-tuple-element.6.crm_ref, f32[256,15]{1,0:T(8,128)S(1)} %get-tuple-element.7.newg_ref), custom_call_target="tpu_custom_call" | custom-call | tf_op jit(solution)/shard_map/pallas_call | solution.py:423

commit v2 on v1

--- a/solution.py
+++ b/solution.py
@@ -10,7 +10,7 @@
 MAXSUB = 8
 GSUB = 4
 LANES = 128
-GROUP = 10
+GROUP = 2
 MESH = pl.DeviceIdType.MESH
 HIGH = lax.Precision.HIGHEST
 F32 = jnp.float32
@@ -151,6 +151,13 @@
             send_sem=crm_send.at[p, peer], recv_sem=crm_recv.at[p, lands],
             device_id={"ha": peer}, device_id_type=MESH)
 
+    def send_pair(p):
+        for reach in range(helpers - 1, 0, -1):
+            for shift in (reach, -reach):
+                @pl.when((ha + shift >= 0) & (ha + shift < helpers))
+                def _():
+                    crm_move(p, lax.rem(ha + shift + helpers, helpers), ha).start()
+
     moves = [[crm_move(p, peer, ha) for peer in peers] for p in range(pairs)]
     arrivals = [[crm_move(p, peer, peer) for peer in peers] for p in range(pairs)]
 
@@ -158,8 +165,7 @@
         copy.wait()
     gather_pair(0)
     pl.semaphore_wait(barrier, len(offsets) + len(peers))
-    for copy in moves[0]:
-        copy.start()
+    send_pair(0)
 
     packed_g[...] = jnp.zeros(packed_g.shape, F32)
     for x in range(tile_x):
@@ -230,8 +236,7 @@
             device_id={"ha": peer}, device_id_type=MESH))
         fmoves[-1].start()
     for p in range(1, pairs):
-        for copy in moves[p]:
-            copy.start()
+        send_pair(p)
     frecv[ha] = fsend[ha]
 
     mix = mixing_ref[...]

time: 36.9 us -> 36.4 us (0.986)
  Pallas kernels: 36.1 us -> 35.6 us
    pallas_call x1, Pallas kernels: 35 us -> 34.6 us  [on_device(): pl.pallas_call(functools.partial(step_kernel, dims, (n_gx, n_gy)), out_sh...]
where the time goes in v2:
time: 36.4 us; the launch traced here: 36.3 us
  Pallas kernels  35.6 us (98%)
  between operations  0.64 us (2%)
    pallas_call x1, Pallas kernels, on_device(): pl.pallas_call(functools.partial(step_kernel, dims, (n_gx, n_gy)), out_sh...  34.6 us
    pallas_call x1, Pallas kernels, on_device(): pl.pallas_call(functools.partial(write_kernel, pieces), out_shape=(jax.Sh...  1.02 us

profile of v2, /device:TPU:0, one launch (start us, length us, event | category | flops | bytes accessed | tf_op | source)
XLA Modules:
  0.0 36.3 jit_solution(10842947106318476295)
XLA Ops:
  0.6 34.6 %shard_map.68 = (f32[60,8,512]{2,1,0:T(8,128)S(1)}, f32[256,15]{1,0:T(8,128)S(1)}) custom-call(s32[4,8]{1,0:T(4,128)} %bitcast.12, s32[4,8]{1,0:T(4,128)} %bitcast.13, f32[8,8]{1,0:T(8,128)} %mixing_ref.1, f32[256,15]{1,0:T(8,128)} %bitcast.11, f32[960,256]{1,0:T(8,128)} %bitcast.10), custom_call_target="tpu_custom_call" | custom-call | tf_op jit(solution)/shard_map/pallas_call | solution.py:393
  35.2 1.0 %shard_map.69 = (f32[60,8,512]{2,1,0:T(8,128)}, f32[256,15]{1,0:T(8,128)}) custom-call(f32[60,8,512]{2,1,0:T(8,128)S(1)} %get-tuple-element.6.crm_ref, f32[256,15]{1,0:T(8,128)S(1)} %get-tuple-element.7.newg_ref), custom_call_target="tpu_custom_call" | custom-call | tf_op jit(solution)/shard_map/pallas_call | solution.py:428
